TPU v7x, 32 devices: a whole 2x2x4 slice. The times are simulated.
32 devices in a mesh: seq: 2 (over core), mp: 4 (over y, x), batch: 4 (over z).
Axes of the slice: x: 2, y: 2, z: 4, core: 2. Of those that a mesh axis runs over, the one named last changes fastest.
Arguments:
- queries: bfloat16 [4, 8, 4096], P('batch', 'seq', 'mp'), may hold values from -6 to 6
- keys: bfloat16 [4, 512, 1024], P('batch', 'seq', 'mp'), may hold values from -6 to 6
- values: bfloat16 [4, 512, 1024], P('batch', 'seq', 'mp'), may hold values from -6 to 6
- key_position: float32 [32, 128], replicated, may hold values from -4 to 4
- compress_keys: bfloat16 [4096, 128], replicated, may hold values from -0.2 to 0.2
- compress_values: bfloat16 [4096, 128], replicated, may hold values from -0.09375 to 0.09375
- out_proj: bfloat16 [4096, 4096], P('mp', 'seq'), may hold values from -0.09375 to 0.09375
- residual: bfloat16 [4, 8, 4096], P(None, None, 'seq'), may hold values from -6 to 6
- norm_gain: float32 [4096], replicated, may hold values from 0.25 to 1.75
- lm_head: bfloat16 [8192, 4096], P(('seq', 'mp', 'batch')), may hold values from -0.4 to 0.4
- targets: int32 [4, 8], replicated, may hold values from 0 to 8191
- lengths: int32 [4], replicated, may hold values from 128 to 512
Outputs:
- token_logprob: float32 [4, 8], P('batch', 'seq')
- rollout_score: float32 [4], P('batch')
All inputs are finite; a program needn't handle non-finite values.
Results may differ from a plain program's by a relative error of at most 0.0005.
The roundings to bfloat16 on the way count: a program that leaves them out, or rounds other values in their place, can miss the bound.
Values may be sent and summed in bfloat16 or wider, within the bound.
No kernel may reach another device: no remote copies, remote signals or barrier semaphores. Data moves between devices by JAX's collectives and lax.ppermute only.
A program may use at most 64 MiB of HBM per device.

v0:
```python
import math
import jax
import jax.numpy as jnp
from jax import lax
from jax.sharding import PartitionSpec as P

HEAD_DIM = 128
BLOCK = 32
STRIDE = 16


def from_behind(block, axis, distance):
    devices = range(lax.axis_size(axis))
    route = [(i - distance, i) for i in devices if i - distance in devices]
    return lax.ppermute(block, axis, route)


def compress_rows(rows, following, position, weight):
    extended = jnp.concatenate([rows, following], 0)
    count = rows.shape[0] // STRIDE
    heads = rows.shape[1] // HEAD_DIM
    shaped = extended.reshape(count + 1, STRIDE, heads, HEAD_DIM)
    blocks = jnp.concatenate([shaped[:-1], shaped[1:]], 1)
    blocks = (blocks.astype(jnp.float32) + position[None, :, None, :]).astype(jnp.bfloat16)
    mapped = jnp.einsum(
        "bjhd,jde->bhe",
        blocks,
        weight.reshape(BLOCK, HEAD_DIM, HEAD_DIM),
        preferred_element_type=jnp.float32,
    )
    return mapped.astype(jnp.bfloat16).reshape(count, heads * HEAD_DIM)


def normalize(hidden, gain):
    widened = hidden.astype(jnp.float32)
    meansq = jnp.mean(widened * widened, -1, keepdims=True)
    return (widened * lax.rsqrt(meansq + 1e-05) * gain).astype(jnp.bfloat16)


def vocab_logits(normed, rows):
    return lax.dot_general(
        normed, rows, (((1,), (1,)), ((), ())), preferred_element_type=jnp.float32
    )


def picked_logit(logits, offset, wanted):
    columns = offset + jnp.arange(logits.shape[1], dtype=jnp.int32)
    hits = columns[None, :] == wanted[:, None]
    return jnp.sum(jnp.where(hits, logits, 0.0), 1)


def body(
    queries,
    keys,
    values,
    key_position,
    compress_keys,
    compress_values,
    out_proj,
    residual,
    norm_gain,
    lm_head,
    targets,
    lengths,
):
    seq_count = lax.axis_size("seq")
    seq_pos = lax.axis_index("seq")
    batch_count = lax.axis_size("batch")
    batch_pos = lax.axis_index("batch")
    qcount = queries.shape[1]
    skip = keys.shape[1] // qcount
    scored = targets.shape[1]
    following = from_behind((keys[0, :STRIDE], values[0, :STRIDE]), "seq", -1)
    comp_keys = compress_rows(keys[0], following[0], key_position, compress_keys)
    comp_values = compress_rows(values[0], following[1], key_position, compress_values)
    every = lax.all_gather(jnp.stack([comp_keys, comp_values], 0), "seq", axis=1, tiled=True)
    heads = keys.shape[2] // HEAD_DIM
    blocks = every.shape[1]
    all_keys = every[0].reshape(blocks, heads, HEAD_DIM)
    all_values = every[1].reshape(blocks, heads, HEAD_DIM)
    group = queries.shape[2] // HEAD_DIM // heads
    query = queries[0].reshape(qcount, heads, group, HEAD_DIM)
    scores = jnp.einsum("qhgd,bhd->qhgb", query, all_keys, preferred_element_type=jnp.float32) * (
        1.0 / math.sqrt(HEAD_DIM)
    )
    index = seq_pos * qcount + jnp.arange(qcount, dtype=jnp.int32)
    limit = index * skip // STRIDE
    visible = (jnp.arange(blocks, dtype=jnp.int32)[None, :] <= limit[:, None])[:, None, None, :]
    scores = jnp.where(visible, scores, -1e30)
    peak = jnp.max(scores, -1, keepdims=True)
    weights = jnp.where(visible, jnp.exp(scores - peak), 0.0)
    probs = (weights / jnp.sum(weights, -1, keepdims=True)).astype(jnp.bfloat16)
    attended = jnp.einsum("qhgb,bhd->qhgd", probs, all_values, preferred_element_type=jnp.float32)
    attended = attended.astype(jnp.bfloat16).reshape(qcount, heads * group * HEAD_DIM)
    spots = jnp.arange(scored, dtype=jnp.int32) * skip + BLOCK - 1
    valid = (spots[None, :] < lengths[:, None]).astype(jnp.float32)
    count = jnp.sum(valid)
    width = out_proj.shape[1]
    rows_all = lax.all_gather(attended, ("seq", "batch"), axis=0, tiled=True)
    part = jnp.dot(rows_all, out_proj, preferred_element_type=jnp.float32)
    summed = lax.psum(part, "mp")
    local_res = (
        residual.reshape(batch_count, seq_count, qcount, width)
        .transpose(1, 0, 2, 3)
        .reshape(-1, width)
    )
    hidden = (local_res.astype(jnp.float32) + summed).astype(jnp.bfloat16)
    whole = lax.all_gather(hidden, "seq", axis=1, tiled=True)
    normed = normalize(whole, norm_gain)
    logits = vocab_logits(normed, lm_head)
    wanted = targets.reshape(batch_count, seq_count, qcount).transpose(1, 0, 2).reshape(-1)
    offset = lax.axis_index(("seq", "mp", "batch")) * lm_head.shape[0]
    picked = picked_logit(logits, offset, wanted)
    local_top = jnp.max(logits, 1)
    top = lax.pmax(local_top, ("seq", "mp", "batch"))
    local_sum = jnp.sum(jnp.exp(logits - top[:, None]), 1)
    total, target_logit = lax.psum((local_sum, picked), ("seq", "mp", "batch"))
    logprob = target_logit - (top + jnp.log(total))
    cube = logprob.reshape(seq_count, batch_count, qcount)
    token_logprob = cube[seq_pos, batch_pos][None, :]
    by_rollout = cube.transpose(1, 0, 2).reshape(batch_count, scored)
    sums = jnp.sum(valid * by_rollout, 1) / count
    rollout_score = sums[batch_pos][None]
    return (token_logprob, rollout_score)


def solution(mesh):
    in_specs = (
        P("batch", "seq", "mp"),
        P("batch", "seq", "mp"),
        P("batch", "seq", "mp"),
        P(),
        P(),
        P(),
        P("mp", "seq"),
        P(None, None, "seq"),
        P(),
        P(("seq", "mp", "batch"), None),
        P(),
        P(),
    )
    out_specs = (P("batch", "seq"), P("batch"))
    return jax.shard_map(body, mesh=mesh, in_specs=in_specs, out_specs=out_specs, check_vma=False)
```

profile of v0, /device:TPU:0, one launch (start us, length us, event | category | flops | bytes accessed | tf_op | source)
XLA Modules:
  0.0 194.4 jit_solution(1485913314387452292)
XLA Ops:
  7.2 0.0 copy-start
  7.2 0.0 copy-start.1
  7.2 0.0 all-reduce.3.cloned.1.call-start
  7.2 0.9 slice_bitcast_fusion.1
  8.1 1.4 collective-permute-start
  9.5 1.3 slice_bitcast_fusion
  10.8 1.3 collective-permute-start.1
  12.1 0.6 iota_compare_fusion
  12.7 0.6 multiply_add_fusion
  13.3 0.9 slice.32
  14.3 0.9 slice.36
  15.2 0.7 copy.47
  15.9 0.1 copy.50
  16.0 1.3 reshape_squeeze.11
  17.3 0.0 collective-permute-done
  17.3 0.9 pad_maximum_fusion.1
  18.2 0.1 copy.48
  18.3 1.6 fusion.6
  19.9 0.0 collective-permute-done.1
  19.9 0.9 pad_maximum_fusion
  20.9 0.0 copy-start.2
  20.9 0.1 copy.51
  21.0 0.0 copy-done.1
  21.0 0.0 copy-start.4
  21.0 0.0 copy-start.6
  21.0 1.0 fusion.7
  22.0 0.0 copy-start.3
  22.1 2.6 %all_gather.9 = bf16[2,32,256]{2,1,0:T(8,128)(2,1)S(1)} all-gather(bf16[2,16,256]{2,1,0:T(8,128)(2,1)S(1)} %pad_maximum_fusion.2), channel_id=1, replica_groups=mesh['seq'=2,'mp'=4,'batch'=4] {'seq'}, dimensions={1}, use_global_device_ids=true | all-gather | bytes 49152 | tf_op jit(solution)/shard_map/all_gather | solution.py:76
  24.7 0.8 fusion.5
  25.5 0.8 fusion.32
  26.4 0.9 fusion.8
  27.3 25.7 %all-gather = bf16[8,4,1024]{2,1,0:T(4,128)(2,1)S(1)} all-gather(bf16[1,4,1024]{2,1,0:T(4,128)(2,1)S(1)} %reshape.113), channel_id=1, replica_groups=mesh['seq'=2,'mp'=4,'batch'=4] {'seq','batch'}, dimensions={0}, use_global_device_ids=true | all-gather | bytes 73728 | tf_op jit(solution)/shard_map/all_gather | solution.py:99
  53.0 0.0 copy-start.5
  53.0 3.7 %fusion.34 = f32[32,2048]{1,0:T(8,128)} fusion(bf16[32,1024]{1,0:T(8,128)(2,1)S(1)} %reshape.114, bf16[1024,2048]{1,0:T(8,128)(2,1)} %param.18), kind=kOutput, calls=%fused_computation.65 | convolution fusion | flops 134217728 | bytes 4521984 | tf_op jit(solution)/shard_map/dot_general | solution.py:100
  56.7 0.0 all-reduce.3.cloned.1.call-update
  56.8 0.0 copy-done.2
  56.8 0.1 reshape.112
  56.9 0.1 reshape.111
  57.0 0.0 copy-done.4
  57.0 0.1 reshape.106
  57.1 0.1 eq.16
  57.2 0.0 copy-done.6
  57.2 0.7 convert_reduce_fusion
  57.9 43.1 %all-reduce.3.cloned.1.call-done = f32[32,2048]{1,0:T(8,128)} async-done(((f32[32,2048]{1,0:T(8,128)}), f32[32,2048]{1,0:T(8,128)}) %all-reduce.3.cloned.1.call-update) | async-done | bytes 262160 | tf_op jit(solution)/shard_map/psum | solution.py:101
  101.0 1.0 add_convert_fusion.4
  102.0 2.0 %all_gather.11 = bf16[32,4096]{1,0:T(8,128)(2,1)S(1)} all-gather(bf16[32,2048]{1,0:T(8,128)(2,1)S(1)} %add_convert_fusion.4), channel_id=1, replica_groups=mesh['seq'=2,'mp'=4,'batch'=4] {'seq'}, dimensions={1}, use_global_device_ids=true | all-gather | bytes 393216 | tf_op jit(solution)/shard_map/all_gather | solution.py:108
  104.0 0.2 fusion.9
  104.1 0.0 copy-done
  104.1 0.0 copy-done.3
  104.2 0.8 fusion.33
  105.0 39.3 %pmax.7 = f32[32]{0:T(128)S(1)} all-reduce(f32[32]{0:T(128)S(1)} %get-tuple-element.8), channel_id=1, replica_groups=mesh['seq'=2,'mp'=4,'batch'=4] {'seq','mp','batch'}, use_global_device_ids=true, to_apply=%region_7.8 | all-reduce | flops 32 | bytes 256 | tf_op jit(solution)/shard_map/pmax | solution.py:115
  144.3 0.2 exponential_reduce_fusion
  144.5 41.0 %all-reduce = (f32[32]{0:T(128)S(1)}, f32[32]{0:T(128)S(1)}) all-reduce(f32[32]{0:T(128)S(1)} %get-tuple-element.3, f32[32]{0:T(128)S(1)} %get-tuple-element.2), channel_id=1, replica_groups=mesh['seq'=2,'mp'=4,'batch'=4] {'seq','mp','batch'}, use_global_device_ids=true, to_apply=%region_5.6 | all-reduce | flops 64 | bytes 512 | tf_op jit(solution)/shard_map/psum | solution.py:117
  185.5 0.1 reshape.110
  185.6 0.0 copy-done.5
  185.6 0.2 fusion.28
  185.8 0.7 broadcast_divide_fusion
  186.4 0.6 dynamic_slice.7
  187.0 0.5 dynamic-slice_bitcast_fusion
  (20 shorter events, 0.2 us)
Async XLA Ops:
  7.2 97.0 %copy-start = (bf16[256,4096]{1,0:T(8,128)(2,1)S(1)}, bf16[256,4096]{1,0:T(8,128)(2,1)}, u32[]{:S(2)}) copy-start(bf16[256,4096]{1,0:T(8,128)(2,1)} %param.21) | copy-start | bytes 6291460
  7.2 13.8 %copy-start.1 = (bf16[4096,128]{1,0:T(8,128)(2,1)S(1)}, bf16[4096,128]{1,0:T(8,128)(2,1)}, u32[]{:S(2)}) copy-start(bf16[4096,128]{1,0:T(8,128)(2,1)} %param.17) | copy-start | bytes 3145732
  7.2 93.8 %all-reduce.3.cloned.1.call-start = ((), (), s32[]{:S(2)}) async-start(), calls=%async_computation | async-start | bytes 524288 | tf_op jit(solution)/shard_map/psum | solution.py:101
  8.1 9.1 %collective-permute-start = (bf16[16,256]{1,0:T(8,128)(2,1)S(1)}, bf16[16,256]{1,0:T(8,128)(2,1)S(1)}, u32[]{:S(2)}, u32[]{:S(2)}) collective-permute-start(bf16[16,256]{1,0:T(8,128)(2,1)S(1)} %slice_bitcast_fusion.1), channel_id=1, source_target_pairs={{16,0},{17,1},{18,2},{19,3},{20,4},{21,5},{22,6},{23,7},{24,8},{25... | collective-permute-start | bytes 24584 | tf_op jit(solution)/shard_map/ppermute | solution.py:15
  10.8 9.1 %collective-permute-start.1 = (bf16[16,256]{1,0:T(8,128)(2,1)}, bf16[16,256]{1,0:T(8,128)(2,1)S(1)}, u32[]{:S(2)}, u32[]{:S(2)}) collective-permute-start(bf16[16,256]{1,0:T(8,128)(2,1)} %slice_bitcast_fusion), channel_id=1, source_target_pairs={{16,0},{17,1},{18,2},{19,3},{20,4},{21,5},{22,6},{23,7},{24,8},{25... | collective-permute-start | bytes 24584 | tf_op jit(solution)/shard_map/ppermute | solution.py:15
  20.9 35.9 %copy-start.2 = (bf16[4,8,2048]{2,1,0:T(8,128)(2,1)S(1)}, bf16[4,8,2048]{2,1,0:T(8,128)(2,1)}, u32[]{:S(2)}) copy-start(bf16[4,8,2048]{2,1,0:T(8,128)(2,1)} %param.19) | copy-start | bytes 393220
  21.0 36.0 %copy-start.4 = (s32[4,8]{1,0:T(4,128)S(1)}, s32[4,8]{1,0:T(4,128)}, u32[]{:S(2)}) copy-start(s32[4,8]{1,0:T(4,128)} %param.22) | copy-start | bytes 388
  21.0 36.2 %copy-start.6 = (s32[4]{0:T(128)S(1)}, s32[4]{0:T(128)}, u32[]{:S(2)}) copy-start(s32[4]{0:T(128)} %param.23) | copy-start | bytes 52
  22.0 82.1 %copy-start.3 = (f32[4096]{0:T(1024)S(1)}, f32[4096]{0:T(1024)}, u32[]{:S(2)}) copy-start(f32[4096]{0:T(1024)} %param.20) | copy-start | bytes 49156
  53.0 132.6 %copy-start.5 = (s32[2,4]{1,0:T(2,128)S(1)}, s32[2,4]{1,0:T(2,128)}, u32[]{:S(2)}) copy-start(s32[2,4]{1,0:T(2,128)} %multiply_add_fusion) | copy-start | bytes 100
Sparse Core Ops, SparseCore 0:
  56.9 44.0 all-reduce.2
where the time goes:
time: 195 us; the launch traced here: 194 us
  blocking collectives  111 us (57%)
  waiting for transfers between devices  43.1 us (22%)
  between operations  14.3 us (7%)
  matrix products  8.86 us (5%)
  local copies, waits for them, and re-layouts  8.01 us (4%)
  other arithmetic  6.72 us (3%)
  starting transfers between devices  2.73 us (1%)
    psum x1, waiting for transfers between devices, body(): summed = lax.psum(part, 'mp')  43.1 us
    psum x1, blocking collectives, body(): total, target_logit = lax.psum((local_sum, picked), ('seq', 'mp', 'batch'))  41 us
    pmax x1, blocking collectives, body(): top = lax.pmax(local_top, ('seq', 'mp', 'batch'))  39.3 us
    all_gather x1, blocking collectives, body(): rows_all = lax.all_gather(attended, ('seq', 'batch'), axis=0, tiled=True)  25.7 us
  transfers between devices with their start and end apart: 3, of which 1 were waited for; matrix products, arithmetic and copies ran while one was open for 5% of the time, Pallas kernels for 0%

commit v1 on v0

--- a/solution.py
+++ b/solution.py
@@ -7,6 +7,27 @@
 HEAD_DIM = 128
 BLOCK = 32
 STRIDE = 16
+
+
+def ring_gather(x, axis, dim):
+    size, index, rows = (lax.axis_size(axis), lax.axis_index(axis), x.shape[dim])
+    forward = [(i, (i + 1) % size) for i in range(size)]
+    behind = [(i, (i - 1) % size) for i in range(size)]
+    filled = jnp.zeros((*x.shape[:dim], size * rows, *x.shape[dim + 1 :]), x.dtype)
+    filled = lax.dynamic_update_slice_in_dim(filled, x, index * rows, axis=dim)
+    from_left = from_right = x
+    halfway = size // 2
+    for step in range(1, halfway + 1):
+        from_left = lax.ppermute(from_left, axis, forward)
+        filled = lax.dynamic_update_slice_in_dim(
+            filled, from_left, (index - step) % size * rows, axis=dim
+        )
+        if step < size - halfway:
+            from_right = lax.ppermute(from_right, axis, behind)
+            filled = lax.dynamic_update_slice_in_dim(
+                filled, from_right, (index + step) % size * rows, axis=dim
+            )
+    return filled
 
 
 def from_behind(block, axis, distance):
@@ -96,7 +117,7 @@
     valid = (spots[None, :] < lengths[:, None]).astype(jnp.float32)
     count = jnp.sum(valid)
     width = out_proj.shape[1]
-    rows_all = lax.all_gather(attended, ("seq", "batch"), axis=0, tiled=True)
+    rows_all = ring_gather(attended, ("seq", "batch"), 0)
     part = jnp.dot(rows_all, out_proj, preferred_element_type=jnp.float32)
     summed = lax.psum(part, "mp")
     local_res = (

time: 195 us -> 189 us (0.969)
  blocking collectives: 111 us -> 85.5 us
  starting transfers between devices: 2.73 us -> 15 us
  waiting for transfers between devices: 43.1 us -> 49 us
    all_gather x1 -> x0, blocking collectives: 25.7 us -> none  [body(): rows_all = lax.all_gather(attended, ('seq', 'batch'), axis=0, tiled=True)]
    ppermute x0 -> x7, starting transfers between devices: none -> 12.3 us  [the longest x3 8.86 us: ring_gather(): from_right = lax.ppermute(from_right, axis, behind)]
    ppermute x0 -> x7, waiting for transfers between devices: none -> 8.62 us  [the longest x4 8.36 us: ring_gather(): from_left = lax.ppermute(from_left, axis, forward)]
    psum x1, waiting for transfers between devices: 43.1 us -> 40.3 us  [body(): summed = lax.psum(part, 'mp')]
  transfers between devices with their start and end apart: 3 -> 10, of which waited for: 1 -> 7; matrix products, arithmetic and copies ran while one was open for 5% -> 6% of each run, Pallas kernels for 0% -> 0%
where the time goes in v1:
time: 189 us; the launch traced here: 188 us
  blocking collectives  85.5 us (45%)
  waiting for transfers between devices  49 us (26%)
  starting transfers between devices  15 us (8%)
  between operations  14.4 us (8%)
  local copies, waits for them, and re-layouts  8.67 us (5%)
  matrix products  8.13 us (4%)
  other arithmetic  7.43 us (4%)
    psum x1, blocking collectives, body(): total, target_logit = lax.psum((local_sum, picked), ('seq', 'mp', 'batch'))  41 us
    psum x1, waiting for transfers between devices, body(): summed = lax.psum(part, 'mp')  40.3 us
    pmax x1, blocking collectives, body(): top = lax.pmax(local_top, ('seq', 'mp', 'batch'))  39.3 us
    ppermute x3, starting transfers between devices, ring_gather(): from_right = lax.ppermute(from_right, axis, behind)  8.86 us
    ppermute x4, waiting for transfers between devices, ring_gather(): from_left = lax.ppermute(from_left, axis, forward)  8.36 us
  transfers between devices with their start and end apart: 10, of which 7 were waited for; matrix products, arithmetic and copies ran while one was open for 6% of the time, Pallas kernels for 0%

profile of v1, /device:TPU:0, one launch (start us, length us, event | category | flops | bytes accessed | tf_op | source)
XLA Modules:
  0.0 188.2 jit_solution(7337722167977617505)
XLA Ops:
  7.2 0.0 copy-start
  7.2 0.0 copy-start.2
  7.2 0.0 all-reduce.3.cloned.1.call-start
  7.2 0.9 slice_bitcast_fusion.1
  8.1 1.4 collective-permute-start
  9.5 1.3 slice_bitcast_fusion
  10.8 1.3 collective-permute-start.1
  12.1 0.6 iota_compare_fusion
  12.7 0.6 multiply_add_fusion
  13.3 0.9 slice.32
  14.2 0.9 slice.36
  15.3 0.7 copy.35
  16.0 0.1 copy.38
  16.0 1.3 reshape_squeeze.11
  17.3 0.0 collective-permute-done
  17.3 0.9 pad_maximum_fusion.1
  18.3 0.1 copy.36
  18.4 1.6 fusion.6
  20.0 0.6 stack_reshape.6
  20.6 0.0 collective-permute-done.1
  20.6 0.9 pad_maximum_fusion
  21.6 0.0 copy-start.3
  21.6 0.1 copy.39
  21.6 0.0 copy-start.5
  21.7 0.0 copy-start.7
  21.7 0.3 fusion.7
  22.0 0.0 copy-start.4
  22.0 0.7 pad_maximum_fusion.2
  22.7 3.2 %all_gather.6 = bf16[2,32,256]{2,1,0:T(8,128)(2,1)S(1)} all-gather(bf16[2,16,256]{2,1,0:T(8,128)(2,1)S(1)} %pad_maximum_fusion.2), channel_id=1, replica_groups=mesh['seq'=2,'mp'=4,'batch'=4] {'seq'}, dimensions={1}, use_global_device_ids=true | all-gather | bytes 49152 | tf_op jit(solution)/shard_map/all_gather | solution.py:97
  25.9 0.8 fusion.5
  26.7 0.8 fusion.33
  27.6 0.9 fusion.8
  28.5 3.1 %collective-permute-start.2 = (bf16[4,1024]{1,0:T(4,128)(2,1)S(1)}, bf16[4,1024]{1,0:T(4,128)(2,1)S(1)}, u32[]{:S(2)}, u32[]{:S(2)}) collective-permute-start(bf16[4,1024]{1,0:T(4,128)(2,1)S(1)} %reshape.109), channel_id=1, source_target_pairs={{0,1},{1,2},{2,3},{3,16},{16,17},{17,18},{18,19},{19,0},{4,5},{5,6... | collective-permute-start | bytes 24584 | tf_op jit(solution)/shard_map/ppermute | solution.py:21
  31.6 2.0 %collective-permute-start.3 = (bf16[4,1024]{1,0:T(4,128)(2,1)S(1)}, bf16[4,1024]{1,0:T(4,128)(2,1)S(1)}, u32[]{:S(2)}, u32[]{:S(2)}) collective-permute-start(bf16[4,1024]{1,0:T(4,128)(2,1)S(1)} %reshape.109), channel_id=1, source_target_pairs={{0,19},{1,0},{2,1},{3,2},{16,3},{17,16},{18,17},{19,18},{4,23},{5,... | collective-permute-start | bytes 24584 | tf_op jit(solution)/shard_map/ppermute | solution.py:26
  33.7 1.2 collective-permute-done.2
  34.9 0.3 collective-permute-start.4
  35.2 0.0 collective-permute-done.3
  35.3 3.3 %collective-permute-start.5 = (bf16[4,1024]{1,0:T(4,128)(2,1)S(1)}, bf16[4,1024]{1,0:T(4,128)(2,1)S(1)}, u32[]{:S(2)}, u32[]{:S(2)}) collective-permute-start(bf16[4,1024]{1,0:T(4,128)(2,1)S(1)} %collective-permute-done.3), channel_id=1, source_target_pairs={{0,19},{1,0},{2,1},{3,2},{16,3},{17,16},{18,17},{19,18},{4,23},{5,... | collective-permute-start | bytes 24584 | tf_op jit(solution)/shard_map/ppermute | solution.py:26
  38.6 1.2 collective-permute-done.4
  39.8 0.1 collective-permute-done.5
  39.9 3.5 %collective-permute-start.7 = (bf16[4,1024]{1,0:T(4,128)(2,1)S(1)}, bf16[4,1024]{1,0:T(4,128)(2,1)S(1)}, u32[]{:S(2)}, u32[]{:S(2)}) collective-permute-start(bf16[4,1024]{1,0:T(4,128)(2,1)S(1)} %collective-permute-done.5), channel_id=1, source_target_pairs={{0,19},{1,0},{2,1},{3,2},{16,3},{17,16},{18,17},{19,18},{4,23},{5,... | collective-permute-start | bytes 24584 | tf_op jit(solution)/shard_map/ppermute | solution.py:26
  43.5 1.2 collective-permute-done.6
  44.7 0.1 collective-permute-done.7
  44.8 4.7 %collective-permute-done.8 = bf16[4,1024]{1,0:T(4,128)(2,1)S(1)} collective-permute-done((bf16[4,1024]{1,0:T(4,128)(2,1)S(1)}, bf16[4,1024]{1,0:T(4,128)(2,1)S(1)}, u32[]{:S(2)}, u32[]{:S(2)}) %collective-permute-start.8) | collective-permute-done | bytes 8224 | tf_op jit(solution)/shard_map/ppermute | solution.py:21
  49.6 3.7 %fusion.35 = f32[32,2048]{1,0:T(8,128)} fusion(bf16[32,1024]{1,0:T(8,128)(2,1)S(1)} %constant_dynamic-update-slice_fusion, bf16[1024,2048]{1,0:T(8,128)(2,1)} %param.18), kind=kOutput, calls=%fused_computation.74 | convolution fusion | flops 134217728 | bytes 4521984 | tf_op jit(solution)/shard_map/dot_general | solution.py:121
  53.3 0.0 all-reduce.3.cloned.1.call-update
  53.3 0.1 reshape.112
  53.4 0.1 reshape.111
  53.6 0.1 reshape.106
  53.6 0.1 eq.24
  53.7 0.7 convert_reduce_fusion
  54.4 40.3 %all-reduce.3.cloned.1.call-done = f32[32,2048]{1,0:T(8,128)} async-done(((f32[32,2048]{1,0:T(8,128)}), f32[32,2048]{1,0:T(8,128)}) %all-reduce.3.cloned.1.call-update) | async-done | bytes 262160 | tf_op jit(solution)/shard_map/psum | solution.py:122
  94.8 1.0 add_convert_fusion.4
  95.7 2.0 %all_gather.7 = bf16[32,4096]{1,0:T(8,128)(2,1)S(1)} all-gather(bf16[32,2048]{1,0:T(8,128)(2,1)S(1)} %add_convert_fusion.4), channel_id=1, replica_groups=mesh['seq'=2,'mp'=4,'batch'=4] {'seq'}, dimensions={1}, use_global_device_ids=true | all-gather | bytes 393216 | tf_op jit(solution)/shard_map/all_gather | solution.py:129
  97.7 0.2 fusion.9
  97.9 0.8 fusion.34
  98.8 39.3 %pmax.7 = f32[32]{0:T(128)S(1)} all-reduce(f32[32]{0:T(128)S(1)} %get-tuple-element.8), channel_id=1, replica_groups=mesh['seq'=2,'mp'=4,'batch'=4] {'seq','mp','batch'}, use_global_device_ids=true, to_apply=%region_7.8 | all-reduce | flops 32 | bytes 256 | tf_op jit(solution)/shard_map/pmax | solution.py:136
  138.1 0.2 exponential_reduce_fusion
  138.3 41.0 %all-reduce = (f32[32]{0:T(128)S(1)}, f32[32]{0:T(128)S(1)}) all-reduce(f32[32]{0:T(128)S(1)} %get-tuple-element.3, f32[32]{0:T(128)S(1)} %get-tuple-element.2), channel_id=1, replica_groups=mesh['seq'=2,'mp'=4,'batch'=4] {'seq','mp','batch'}, use_global_device_ids=true, to_apply=%region_5.6 | all-reduce | flops 64 | bytes 512 | tf_op jit(solution)/shard_map/psum | solution.py:138
  179.3 0.1 reshape.110
  179.4 0.2 fusion.28
  179.5 0.7 broadcast_divide_fusion
  180.2 0.6 dynamic_slice.7
  180.8 0.5 fusion.29
  (38 shorter events, 0.3 us)
Async XLA Ops:
  7.2 90.8 %copy-start = (bf16[256,4096]{1,0:T(8,128)(2,1)S(1)}, bf16[256,4096]{1,0:T(8,128)(2,1)}, u32[]{:S(2)}) copy-start(bf16[256,4096]{1,0:T(8,128)(2,1)} %param.21) | copy-start | bytes 6291460
  7.2 14.5 %copy-start.2 = (f32[32,128]{1,0:T(8,128)S(1)}, f32[32,128]{1,0:T(8,128)}, u32[]{:S(2)}) copy-start(f32[32,128]{1,0:T(8,128)} %param.15) | copy-start | bytes 49156
  7.2 14.5 %copy-start.1 = (bf16[4096,128]{1,0:T(8,128)(2,1)S(1)}, bf16[4096,128]{1,0:T(8,128)(2,1)}, u32[]{:S(2)}) copy-start(bf16[4096,128]{1,0:T(8,128)(2,1)} %param.17) | copy-start | bytes 3145732
  7.2 87.6 %all-reduce.3.cloned.1.call-start = ((), (), s32[]{:S(2)}) async-start(), calls=%async_computation | async-start | bytes 524288 | tf_op jit(solution)/shard_map/psum | solution.py:122
  8.1 9.2 %collective-permute-start = (bf16[16,256]{1,0:T(8,128)(2,1)S(1)}, bf16[16,256]{1,0:T(8,128)(2,1)S(1)}, u32[]{:S(2)}, u32[]{:S(2)}) collective-permute-start(bf16[16,256]{1,0:T(8,128)(2,1)S(1)} %slice_bitcast_fusion.1), channel_id=1, source_target_pairs={{16,0},{17,1},{18,2},{19,3},{20,4},{21,5},{22,6},{23,7},{24,8},{25... | collective-permute-start | bytes 24584 | tf_op jit(solution)/shard_map/ppermute | solution.py:36
  10.8 9.8 %collective-permute-start.1 = (bf16[16,256]{1,0:T(8,128)(2,1)}, bf16[16,256]{1,0:T(8,128)(2,1)}, u32[]{:S(2)}, u32[]{:S(2)}) collective-permute-start(bf16[16,256]{1,0:T(8,128)(2,1)} %slice_bitcast_fusion), channel_id=1, source_target_pairs={{16,0},{17,1},{18,2},{19,3},{20,4},{21,5},{22,6},{23,7},{24,8},{25... | collective-permute-start | bytes 24584 | tf_op jit(solution)/shard_map/ppermute | solution.py:36
  21.6 31.7 %copy-start.3 = (bf16[4,8,2048]{2,1,0:T(8,128)(2,1)S(1)}, bf16[4,8,2048]{2,1,0:T(8,128)(2,1)}, u32[]{:S(2)}) copy-start(bf16[4,8,2048]{2,1,0:T(8,128)(2,1)} %param.19) | copy-start | bytes 393220
  21.6 31.9 %copy-start.5 = (s32[4,8]{1,0:T(4,128)S(1)}, s32[4,8]{1,0:T(4,128)}, u32[]{:S(2)}) copy-start(s32[4,8]{1,0:T(4,128)} %param.22) | copy-start | bytes 388
  21.7 32.1 %copy-start.7 = (s32[4]{0:T(128)S(1)}, s32[4]{0:T(128)}, u32[]{:S(2)}) copy-start(s32[4]{0:T(128)} %param.23) | copy-start | bytes 52
  22.0 76.0 %copy-start.4 = (f32[4096]{0:T(1024)S(1)}, f32[4096]{0:T(1024)}, u32[]{:S(2)}) copy-start(f32[4096]{0:T(1024)} %param.20) | copy-start | bytes 49156
  28.5 6.4 %collective-permute-start.2 = (bf16[4,1024]{1,0:T(4,128)(2,1)S(1)}, bf16[4,1024]{1,0:T(4,128)(2,1)S(1)}, u32[]{:S(2)}, u32[]{:S(2)}) collective-permute-start(bf16[4,1024]{1,0:T(4,128)(2,1)S(1)} %reshape.109), channel_id=1, source_target_pairs={{0,1},{1,2},{2,3},{3,16},{16,17},{17,18},{18,19},{19,0},{4,5},{5,6... | collective-permute-start | bytes 24584 | tf_op jit(solution)/shard_map/ppermute | solution.py:21
  31.6 3.7 %collective-permute-start.3 = (bf16[4,1024]{1,0:T(4,128)(2,1)S(1)}, bf16[4,1024]{1,0:T(4,128)(2,1)S(1)}, u32[]{:S(2)}, u32[]{:S(2)}) collective-permute-start(bf16[4,1024]{1,0:T(4,128)(2,1)S(1)} %reshape.109), channel_id=1, source_target_pairs={{0,19},{1,0},{2,1},{3,2},{16,3},{17,16},{18,17},{19,18},{4,23},{5,... | collective-permute-start | bytes 24584 | tf_op jit(solution)/shard_map/ppermute | solution.py:26
  34.9 4.9 %collective-permute-start.4 = (bf16[4,1024]{1,0:T(4,128)(2,1)S(1)}, bf16[4,1024]{1,0:T(4,128)(2,1)S(1)}, u32[]{:S(2)}, u32[]{:S(2)}) collective-permute-start(bf16[4,1024]{1,0:T(4,128)(2,1)S(1)} %collective-permute-done.2), channel_id=1, source_target_pairs={{0,1},{1,2},{2,3},{3,16},{16,17},{17,18},{18,19},{19,0},{4,5},{5,6... | collective-permute-start | bytes 24584 | tf_op jit(solution)/shard_map/ppermute | solution.py:21
  35.3 4.7 %collective-permute-start.5 = (bf16[4,1024]{1,0:T(4,128)(2,1)S(1)}, bf16[4,1024]{1,0:T(4,128)(2,1)S(1)}, u32[]{:S(2)}, u32[]{:S(2)}) collective-permute-start(bf16[4,1024]{1,0:T(4,128)(2,1)S(1)} %collective-permute-done.3), channel_id=1, source_target_pairs={{0,19},{1,0},{2,1},{3,2},{16,3},{17,16},{18,17},{19,18},{4,23},{5,... | collective-permute-start | bytes 24584 | tf_op jit(solution)/shard_map/ppermute | solution.py:26
  39.8 4.9 %collective-permute-start.6 = (bf16[4,1024]{1,0:T(4,128)(2,1)S(1)}, bf16[4,1024]{1,0:T(4,128)(2,1)S(1)}, u32[]{:S(2)}, u32[]{:S(2)}) collective-permute-start(bf16[4,1024]{1,0:T(4,128)(2,1)S(1)} %collective-permute-done.4), channel_id=1, source_target_pairs={{0,1},{1,2},{2,3},{3,16},{16,17},{17,18},{18,19},{19,0},{4,5},{5,6... | collective-permute-start | bytes 24584 | tf_op jit(solution)/shard_map/ppermute | solution.py:21
  39.9 4.9 %collective-permute-start.7 = (bf16[4,1024]{1,0:T(4,128)(2,1)S(1)}, bf16[4,1024]{1,0:T(4,128)(2,1)S(1)}, u32[]{:S(2)}, u32[]{:S(2)}) collective-permute-start(bf16[4,1024]{1,0:T(4,128)(2,1)S(1)} %collective-permute-done.5), channel_id=1, source_target_pairs={{0,19},{1,0},{2,1},{3,2},{16,3},{17,16},{18,17},{19,18},{4,23},{5,... | collective-permute-start | bytes 24584 | tf_op jit(solution)/shard_map/ppermute | solution.py:26
  44.7 4.9 %collective-permute-start.8 = (bf16[4,1024]{1,0:T(4,128)(2,1)S(1)}, bf16[4,1024]{1,0:T(4,128)(2,1)S(1)}, u32[]{:S(2)}, u32[]{:S(2)}) collective-permute-start(bf16[4,1024]{1,0:T(4,128)(2,1)S(1)} %collective-permute-done.6), channel_id=1, source_target_pairs={{0,1},{1,2},{2,3},{3,16},{16,17},{17,18},{18,19},{19,0},{4,5},{5,6... | collective-permute-start | bytes 24584 | tf_op jit(solution)/shard_map/ppermute | solution.py:21
  49.5 129.8 %copy-start.6 = (s32[2,4]{1,0:T(2,128)S(1)}, s32[2,4]{1,0:T(2,128)}, u32[]{:S(2)}) copy-start(s32[2,4]{1,0:T(2,128)} %multiply_add_fusion) | copy-start | bytes 100
Sparse Core Ops, SparseCore 0:
  53.4 41.2 all-reduce.2
